TPU v7x, 32 devices: a whole 2x2x4 slice. The times are simulated.
32 devices in a mesh: row: 8 (over z, x), col: 4 (over y, core).
Axes of the slice: x: 2, y: 2, z: 4, core: 2. Of those that a mesh axis runs over, the one named last changes fastest.
Arguments:
- trailing: float32 [16384, 8192], P('row', 'col'), may hold values from -6 to 6
- vectors: float32 [16384, 256], P(('row', 'col')), may hold values from -0.1875 to 0.1875
- tfactor: float32 [256, 256], replicated, may hold values from -0.375 to 0.375
Outputs:
- updated: float32 [16384, 8192], P('row', 'col')
All inputs are finite; a program needn't handle non-finite values.
Results may differ from a plain program's by a relative error of at most 0.0003.
Values sent between devices are 32-bit elements.
A program may use at most 128 MiB of HBM per device.

v0:
```python
import jax
import jax.numpy as jnp
from jax import lax
from jax.sharding import PartitionSpec as P


def shards(trailing, vectors, tfactor):
    high = lax.Precision.HIGHEST
    near_vectors = lax.all_gather(vectors, "col", axis=0, tiled=True)
    partial_value = jnp.dot(
        near_vectors.T, trailing, precision=high, preferred_element_type=jnp.float32
    )
    summed = lax.psum(partial_value, "row")
    scaled = jnp.dot(tfactor, summed, precision=high, preferred_element_type=jnp.float32)
    change = jnp.dot(near_vectors, scaled, precision=high, preferred_element_type=jnp.float32)
    return trailing - change


def solution(mesh):
    placed = (P("row", "col"), P(("row", "col"), None), P())
    return jax.shard_map(
        shards, mesh=mesh, in_specs=placed, out_specs=P("row", "col"), check_vma=False
    )
```

profile of v0, /device:TPU:0, one launch (start us, length us, event | category | flops | bytes accessed | tf_op | source)
XLA Modules:
  0.0 203.2 jit_solution(18051398769543396435)
XLA Ops:
  6.5 0.0 copy-start
  6.5 0.0 all-gather.2.cloned.1.call-start
  6.5 0.7 all-gather.2.cloned.1.call-update
  7.3 0.0 all-reduce.2.cloned.1.call-start
  7.3 26.9 %all-gather.2.cloned.1.call-done = f32[2048,256]{1,0:T(8,128)} async-done(((f32[512,256]{1,0:T(8,128)}), f32[2048,256]{1,0:T(8,128)}) %all-gather.2.cloned.1.call-update) | async-done | bytes 2097168 | tf_op jit(solution)/shard_map/all_gather | solution.py:9
  34.2 18.3 %fusion = f32[256,2048]{1,0:T(8,128)} fusion(f32[2048,256]{1,0:T(8,128)} %all-gather.2.cloned.1.call-done, f32[2048,2048]{1,0:T(8,128)} %param.3), kind=kOutput, calls=%fused_computation.1 | convolution fusion | flops 12884901888 | bytes 20971520 | tf_op jit(solution)/shard_map/dot_general | solution.py:10
  52.5 0.0 all-reduce.2.cloned.1.call-update
  52.5 17.7 %copy.4 = f32[2048,2048]{0,1:T(8,128)} copy(f32[2048,2048]{1,0:T(8,128)} %param.3) | data formatting | bytes 33554432 | tf_op args[0]
  70.2 0.0 copy-start.2
  70.2 84.8 %all-reduce.2.cloned.1.call-done = f32[256,2048]{1,0:T(8,128)} async-done(((f32[256,2048]{1,0:T(8,128)}), f32[256,2048]{1,0:T(8,128)}) %all-reduce.2.cloned.1.call-update) | async-done | bytes 2097168 | tf_op jit(solution)/shard_map/psum | solution.py:13
  155.0 0.0 copy-done
  155.0 5.2 %fusion.1 = f32[2048,256]{1,0:T(8,128)S(1)} fusion(f32[256,2048]{1,0:T(8,128)} %all-reduce.2.cloned.1.call-done, f32[256,256]{1,0:T(8,128)S(1)} %copy-done), kind=kOutput, calls=%fused_computation.2 | convolution fusion | flops 1610612736 | bytes 4456448 | tf_op jit(solution)/shard_map/dot_general | solution.py:14
  160.2 0.0 copy-done.2
  160.2 18.5 %bitcast_subtract_fusion = f32[2048,2048]{0,1:T(8,128)} fusion(f32[2048,2048]{0,1:T(8,128)} %copy.4, f32[2048,256]{1,0:T(8,128)S(1)} %fusion.1, f32[2048,256]{1,0:T(8,128)S(1)} %copy-done.2), kind=kOutput, calls=%fused_computation | convolution fusion | flops 12889096192 | bytes 37748736 | tf_op jit(solution)/shard_map/dot_general | solution.py:15
  178.7 0.0 copy-start.1
  178.7 17.6 %copy.5 = f32[2048,2048]{1,0:T(8,128)} copy(f32[2048,2048]{0,1:T(8,128)} %bitcast_subtract_fusion) | data formatting | bytes 33554432 | tf_op jit(solution)/shard_map/sub | solution.py:16
  196.3 0.0 copy-done.1
Async XLA Ops:
  6.5 148.5 %copy-start = (f32[256,256]{1,0:T(8,128)S(1)}, f32[256,256]{1,0:T(8,128)}, u32[]{:S(2)}) copy-start(f32[256,256]{1,0:T(8,128)} %param.5) | copy-start | bytes 786436
  6.5 27.7 %all-gather.2.cloned.1.call-start = ((), (), s32[]{:S(2)}) async-start(), calls=%async_computation | async-start | bytes 2621440 | tf_op jit(solution)/shard_map/all_gather | solution.py:9
  7.3 147.7 %all-reduce.2.cloned.1.call-start = ((), (), s32[]{:S(2)}) async-start(), calls=%async_computation.1 | async-start | bytes 4194304 | tf_op jit(solution)/shard_map/psum | solution.py:13
  70.2 90.0 %copy-start.2 = (f32[2048,256]{1,0:T(8,128)S(1)}, f32[2048,256]{1,0:T(8,128)}, u32[]{:S(2)}) copy-start(f32[2048,256]{1,0:T(8,128)} %all-gather.2.cloned.1.call-done) | copy-start | bytes 6291460
  178.7 17.6 %copy-start.1 = (f32[256,256]{1,0:T(8,128)S(1)}, f32[256,256]{1,0:T(8,128)}, u32[]{:S(2)}) copy-start(f32[256,256]{1,0:T(8,128)} %param.5) | copy-start | bytes 786436
Sparse Core Ops, SparseCore 0:
  8.9 25.2 all-gather.1
  52.7 102.2 all-reduce.1
where the time goes:
time: 204 us; the launch traced here: 203 us
  waiting for transfers between devices  112 us (55%)
  matrix products  42 us (21%)
  local copies, waits for them, and re-layouts  35.3 us (17%)
  between operations  13.4 us (7%)
    psum x1, waiting for transfers between devices, shards(): summed = lax.psum(partial_value, 'row')  84.8 us
    all_gather x1, waiting for transfers between devices, shards(): near_vectors = lax.all_gather(vectors, 'col', axis=0, tiled=True)  26.9 us
    dot_general x1, matrix products, shards(): jnp.dot(near_vectors, scaled, precision=high, preferred_element_type=jnp....  18.5 us
    dot_general x1, matrix products, shards(): jnp.dot(near_vectors.T, trailing, precision=high, preferred_element_type=...  18.3 us
    unnamed x7, local copies, waits for them, and re-layouts  17.7 us
    sub x1, local copies, waits for them, and re-layouts, shards(): return trailing - change  17.6 us
    dot_general x1, matrix products, shards(): jnp.dot(tfactor, summed, precision=high, preferred_element_type=jnp.float32)  5.17 us
  transfers between devices with their start and end apart: 2, of which 2 were waited for; matrix products, arithmetic and copies ran while one was open for 9% of the time, Pallas kernels for 0%

commit v1 on v0

--- a/solution.py
+++ b/solution.py
@@ -2,6 +2,15 @@
 import jax.numpy as jnp
 from jax import lax
 from jax.sharding import PartitionSpec as P
+
+
+def add_in_pairs(x, axis):
+    size = lax.axis_size(axis)
+    result, far = (x, 1)
+    while far < size:
+        result = result + lax.ppermute(result, axis, [(i, i ^ far) for i in range(size)])
+        far = 2 * far
+    return result
 
 
 def shards(trailing, vectors, tfactor):
@@ -10,7 +19,7 @@
     partial_value = jnp.dot(
         near_vectors.T, trailing, precision=high, preferred_element_type=jnp.float32
     )
-    summed = lax.psum(partial_value, "row")
+    summed = add_in_pairs(partial_value, "row")
     scaled = jnp.dot(tfactor, summed, precision=high, preferred_element_type=jnp.float32)
     change = jnp.dot(near_vectors, scaled, precision=high, preferred_element_type=jnp.float32)
     return trailing - change

time: 204 us -> 288 us (1.41)
  waiting for transfers between devices: 112 us -> 191 us
  starting transfers between devices: 0.04 us -> 5.57 us
    ppermute x0 -> x3, waiting for transfers between devices: none -> 164 us  [add_in_pairs(): lax.ppermute(result, axis, [(i, i ^ far) for i in range(size)])]
    psum x1 -> x0, waiting for transfers between devices: 84.8 us -> none  [shards(): summed = lax.psum(partial_value, 'row')]
    ppermute x0 -> x3, starting transfers between devices: none -> 5.57 us  [add_in_pairs(): lax.ppermute(result, axis, [(i, i ^ far) for i in range(size)])]
  transfers between devices with their start and end apart: 2 -> 4, of which waited for: 2 -> 4; matrix products, arithmetic and copies ran while one was open for 9% -> 6% of each run, Pallas kernels for 0% -> 0%
where the time goes in v1:
time: 288 us; the launch traced here: 287 us
  waiting for transfers between devices  191 us (66%)
  matrix products  40.7 us (14%)
  local copies, waits for them, and re-layouts  35.2 us (12%)
  between operations  13.4 us (5%)
  starting transfers between devices  5.57 us (2%)
    ppermute x3, waiting for transfers between devices, add_in_pairs(): lax.ppermute(result, axis, [(i, i ^ far) for i in range(size)])  164 us
    all_gather x1, waiting for transfers between devices, shards(): near_vectors = lax.all_gather(vectors, 'col', axis=0, tiled=True)  27 us
    dot_general x1, matrix products, shards(): jnp.dot(near_vectors, scaled, precision=high, preferred_element_type=jnp....  18.5 us
    sub x1, local copies, waits for them, and re-layouts, shards(): return trailing - change  17.6 us
    unnamed x7, local copies, waits for them, and re-layouts  17.6 us
    dot_general x1, matrix products, shards(): jnp.dot(near_vectors.T, trailing, precision=high, preferred_element_type=...  17 us
  transfers between devices with their start and end apart: 4, of which 4 were waited for; matrix products, arithmetic and copies ran while one was open for 6% of the time, Pallas kernels for 0%

profile of v1, /device:TPU:0, one launch (start us, length us, event | category | flops | bytes accessed | tf_op | source)
XLA Modules:
  0.0 286.9 jit_solution(4681599309310762461)
XLA Ops:
  6.5 0.0 copy-start
  6.5 0.0 all-gather.2.cloned.1.call-start
  6.5 0.7 all-gather.2.cloned.1.call-update
  7.3 27.0 %all-gather.2.cloned.1.call-done = f32[2048,256]{1,0:T(8,128)} async-done(((f32[512,256]{1,0:T(8,128)}), f32[2048,256]{1,0:T(8,128)}) %all-gather.2.cloned.1.call-update) | async-done | bytes 2097168 | tf_op jit(solution)/shard_map/all_gather | solution.py:18
  34.2 17.0 %fusion.2 = f32[256,2048]{1,0:T(8,128)S(1)} fusion(f32[2048,256]{1,0:T(8,128)} %all-gather.2.cloned.1.call-done, f32[2048,2048]{1,0:T(8,128)} %param.3), kind=kOutput, calls=%fused_computation.3 | convolution fusion | flops 12884901888 | bytes 20971520 | tf_op jit(solution)/shard_map/dot_general | solution.py:19
  51.3 1.5 collective-permute-start
  52.8 46.3 %collective-permute-done = f32[256,2048]{1,0:T(8,128)S(1)} collective-permute-done((f32[256,2048]{1,0:T(8,128)S(1)}, f32[256,2048]{1,0:T(8,128)S(1)}, u32[]{:S(2)}, u32[]{:S(2)}) %collective-permute-start) | collective-permute-done | bytes 2097184 | tf_op jit(solution)/shard_map/ppermute | solution.py:11
  99.1 0.3 add.9
  99.4 1.6 collective-permute-start.1
  100.9 45.4 %collective-permute-done.1 = f32[256,2048]{1,0:T(8,128)S(1)} collective-permute-done((f32[256,2048]{1,0:T(8,128)S(1)}, f32[256,2048]{1,0:T(8,128)S(1)}, u32[]{:S(2)}, u32[]{:S(2)}) %collective-permute-start.1) | collective-permute-done | bytes 2097184 | tf_op jit(solution)/shard_map/ppermute | solution.py:11
  146.4 0.3 add.10
  146.6 2.5 collective-permute-start.2
  149.1 17.6 %copy.4 = f32[2048,2048]{0,1:T(8,128)} copy(f32[2048,2048]{1,0:T(8,128)} %param.3) | data formatting | bytes 33554432 | tf_op args[0]
  166.7 0.0 copy-start.2
  166.7 72.0 %collective-permute-done.2 = f32[256,2048]{1,0:T(8,128)} collective-permute-done((f32[256,2048]{1,0:T(8,128)S(1)}, f32[256,2048]{1,0:T(8,128)}, u32[]{:S(2)}, u32[]{:S(2)}) %collective-permute-start.2) | collective-permute-done | bytes 2097184 | tf_op jit(solution)/shard_map/ppermute | solution.py:11
  238.7 0.0 copy-done
  238.7 5.2 %fusion = f32[2048,256]{1,0:T(8,128)S(1)} fusion(f32[256,256]{1,0:T(8,128)S(1)} %copy-done, f32[256,2048]{1,0:T(8,128)S(1)} %add.10, f32[256,2048]{1,0:T(8,128)} %collective-permute-done.2), kind=kOutput, calls=%fused_computation.1 | convolution fusion | flops 1611137024 | bytes 6553600 | tf_op jit(solution)/shard_map/dot_general | solution.py:23
  243.9 0.0 copy-done.2
  243.9 18.5 %bitcast_subtract_fusion = f32[2048,2048]{0,1:T(8,128)} fusion(f32[2048,2048]{0,1:T(8,128)} %copy.4, f32[2048,256]{1,0:T(8,128)S(1)} %fusion, f32[2048,256]{1,0:T(8,128)S(1)} %copy-done.2), kind=kOutput, calls=%fused_computation | convolution fusion | flops 12889096192 | bytes 37748736 | tf_op jit(solution)/shard_map/dot_general | solution.py:24
  262.4 0.0 copy-start.1
  262.4 17.6 %copy.5 = f32[2048,2048]{1,0:T(8,128)} copy(f32[2048,2048]{0,1:T(8,128)} %bitcast_subtract_fusion) | data formatting | bytes 33554432 | tf_op jit(solution)/shard_map/sub | solution.py:25
  280.0 0.0 copy-done.1
Async XLA Ops:
  6.5 232.2 %copy-start = (f32[256,256]{1,0:T(8,128)S(1)}, f32[256,256]{1,0:T(8,128)}, u32[]{:S(2)}) copy-start(f32[256,256]{1,0:T(8,128)} %param.5) | copy-start | bytes 786436
  6.5 27.7 %all-gather.2.cloned.1.call-start = ((), (), s32[]{:S(2)}) async-start(), calls=%async_computation | async-start | bytes 2621440 | tf_op jit(solution)/shard_map/all_gather | solution.py:18
  51.3 47.8 %collective-permute-start = (f32[256,2048]{1,0:T(8,128)S(1)}, f32[256,2048]{1,0:T(8,128)S(1)}, u32[]{:S(2)}, u32[]{:S(2)}) collective-permute-start(f32[256,2048]{1,0:T(8,128)S(1)} %fusion.2), channel_id=1, source_target_pairs={{0,4},{4,0},{8,12},{12,8},{16,20},{20,16},{24,28},{28,24},{1,5},{5... | collective-permute-start | bytes 6291464 | tf_op jit(solution)/shard_map/ppermute | solution.py:11
  99.4 47.0 %collective-permute-start.1 = (f32[256,2048]{1,0:T(8,128)S(1)}, f32[256,2048]{1,0:T(8,128)S(1)}, u32[]{:S(2)}, u32[]{:S(2)}) collective-permute-start(f32[256,2048]{1,0:T(8,128)S(1)} %add.9), channel_id=1, source_target_pairs={{0,8},{4,12},{8,0},{12,4},{16,24},{20,28},{24,16},{28,20},{1,9},{5... | collective-permute-start | bytes 6291464 | tf_op jit(solution)/shard_map/ppermute | solution.py:11
  146.6 92.1 %collective-permute-start.2 = (f32[256,2048]{1,0:T(8,128)S(1)}, f32[256,2048]{1,0:T(8,128)}, u32[]{:S(2)}, u32[]{:S(2)}) collective-permute-start(f32[256,2048]{1,0:T(8,128)S(1)} %add.10), channel_id=1, source_target_pairs={{0,16},{4,20},{8,24},{12,28},{16,0},{20,4},{24,8},{28,12},{1,17},{... | collective-permute-start | bytes 6291464 | tf_op jit(solution)/shard_map/ppermute | solution.py:11
  166.7 77.2 %copy-start.2 = (f32[2048,256]{1,0:T(8,128)S(1)}, f32[2048,256]{1,0:T(8,128)}, u32[]{:S(2)}) copy-start(f32[2048,256]{1,0:T(8,128)} %all-gather.2.cloned.1.call-done) | copy-start | bytes 6291460
  262.4 17.6 %copy-start.1 = (f32[256,256]{1,0:T(8,128)S(1)}, f32[256,256]{1,0:T(8,128)}, u32[]{:S(2)}) copy-start(f32[256,256]{1,0:T(8,128)} %param.5) | copy-start | bytes 786436
Sparse Core Ops, SparseCore 0:
  8.9 25.2 all-gather.1
